TPU v7x, 512 devices: a whole 4x8x8 slice. The times are simulated.
512 devices in a mesh: heads: 8 (over y_lo, x), blk: 64 (over y_hi, z, core).
Axes of the slice: x: 4, y: 8 (y_hi: 4, y_lo: 2; y = y_hi * 2 + y_lo), z: 8, core: 2. Of those that a mesh axis runs over, the one named last changes fastest.
Arguments:
- queries: bfloat16 [4096, 64, 128], P('blk', 'heads'), may hold values from -8 to 8
- prefix_keys: bfloat16 [8, 131072, 128], P('heads', 'blk'), may hold values from -8 to 8
- cached_prefix_values: bfloat16 [8, 131072, 128], P('heads', 'blk'), may hold values from -6 to 6
- shard_len: int32 [64], replicated, may hold values from 512 to 2048
- reach: int32 [64], replicated, may hold values from 4096 to 8192
- w_out: bfloat16 [8192, 16384], P('heads', 'blk'), may hold values from -0.0625 to 0.0625
Outputs:
- projected: bfloat16 [4096, 16384], P('heads', 'blk')
All inputs are finite; a program needn't handle non-finite values.
Results may differ from a plain program's by a relative error of at most 0.0056.
Values may be sent and summed in bfloat16 or wider, within the bound.
No kernel may reach another device: no remote copies, remote signals or barrier semaphores. Data moves between devices by JAX's collectives and lax.ppermute only.
A program may use at most 64 MiB of HBM per device.

v0:
```python
import jax
import jax.numpy as jnp
from jax import lax
from jax.sharding import Mesh
from jax.sharding import PartitionSpec as P

SPAN = 4
HEADS = ("heads_0", "heads_1")
masked_score = -1e30


def passed_along(value, axis, steps):
    count = lax.axis_size(axis)
    pairs = [(source, (source + steps) % count) for source in range(count)]
    return lax.ppermute(value, axis, pairs)


def split_up(value, dim, length):
    lengths = value.shape
    blocks = value.reshape(*lengths[:dim], length, lengths[dim] // length, *lengths[dim + 1 :])
    return jnp.moveaxis(blocks, dim, 0)


def joined_along(blocks, dim):
    lengths = list(blocks.shape[1:])
    lengths[dim] *= blocks.shape[0]
    return jnp.moveaxis(blocks, 0, dim).reshape(lengths)


def exchange_in_order(blocks, axes, turns):
    lengths = [lax.axis_size(a) for a in axes]
    blocks = blocks.reshape(*lengths, *blocks.shape[1:])
    for k in turns:
        blocks = lax.all_to_all(blocks, axes[k], split_axis=k, concat_axis=k, tiled=True)
    return blocks.reshape(-1, *blocks.shape[len(axes) :])


def stepwise_exchange(value, axes, turns, split_dim, concat_dim):
    blocks = split_up(value, split_dim, lax.axis_size(axes))
    return joined_along(exchange_in_order(blocks, axes, turns), concat_dim)


def part_stats(query_tile_rows, key_block, value_block, visible):
    head_size = query_tile_rows.shape[-1]
    scores = jnp.einsum(
        "thgd,hnd->thgn", query_tile_rows, key_block, preferred_element_type=jnp.float32
    ) * head_size ** (-0.5)
    visible_grid = visible[:, None, None, :]
    maxima = jnp.max(jnp.where(visible_grid, scores, masked_score), axis=-1)
    weights = jnp.where(visible_grid, jnp.exp(scores - maxima[..., None]), 0.0)
    totals = jnp.sum(weights, axis=-1)
    weighted = jnp.einsum(
        "thgn,hnd->thgd",
        weights.astype(jnp.bfloat16),
        value_block,
        preferred_element_type=jnp.float32,
    )
    return (maxima, totals, weighted)


def combine_parts(first, second):
    joined = jnp.maximum(first[0], second[0])
    first_factor = jnp.exp(first[0] - joined)
    second_factor = jnp.exp(second[0] - joined)
    totals = first[1] * first_factor + second[1] * second_factor
    weighted = first[2] * first_factor[..., None] + second[2] * second_factor[..., None]
    return (joined, totals, weighted)


def on_device(queries, prefix_keys, cached_prefix_values, shard_len, reach, w_out):
    shard_count = lax.axis_size("blk")
    group_count = lax.axis_size(HEADS)
    own_index = lax.axis_index("blk")
    query_len = queries.shape[0]
    heads_local = queries.shape[1]
    head_size = queries.shape[2]
    kv_local = prefix_keys.shape[0]
    keys_len = prefix_keys.shape[1]
    columns = w_out.shape[1]
    full_weight = lax.all_gather(w_out, HEADS, axis=0, tiled=True)
    local_queries = queries.reshape(query_len, kv_local, heads_local // kv_local, head_size)
    row_ids = jnp.arange(query_len, dtype=jnp.int32)[:, None]
    slot_ids = jnp.arange(keys_len, dtype=jnp.int32)[None, :]

    def mask_for(block_id, shard_id, offset):
        return (slot_ids < shard_len[shard_id]) & (
            offset * keys_len + slot_ids < reach[block_id] + row_ids
        )

    running = part_stats(
        local_queries, prefix_keys, cached_prefix_values, mask_for(own_index, own_index, 0)
    )
    for offset in range(1, SPAN):
        visitor = passed_along(local_queries, "blk", offset)
        owner_id = (own_index - offset + shard_count) % shard_count
        maxima, totals, weighted = part_stats(
            visitor, prefix_keys, cached_prefix_values, mask_for(owner_id, own_index, offset)
        )
        returned = passed_along((maxima, totals, weighted), "blk", -offset)
        running = combine_parts(running, returned)
    attended = (
        (running[2] / running[1][..., None])
        .astype(jnp.bfloat16)
        .reshape(query_len, heads_local * head_size)
    )
    share_rows = stepwise_exchange(attended, HEADS, (0, 1), 0, 1)
    strided = jnp.dot(
        lax.all_gather(share_rows, "blk", axis=0, tiled=True),
        full_weight,
        preferred_element_type=jnp.float32,
    ).astype(jnp.bfloat16)
    share_len = share_rows.shape[0]
    grouped = strided.reshape(group_count, shard_count // group_count, 1, share_len, columns)
    ordered = lax.all_to_all(grouped, HEADS, split_axis=0, concat_axis=2, tiled=True)
    return ordered.reshape(shard_count // group_count * group_count * share_len, columns)


def solution(mesh):
    finer = Mesh(mesh.devices.reshape(2, 4, mesh.shape["blk"]), ("heads_0", "heads_1", "blk"))
    placed = (
        P("blk", HEADS, None),
        P(HEADS, "blk", None),
        P(HEADS, "blk", None),
        P(),
        P(),
        P(HEADS, "blk"),
    )
    return jax.shard_map(
        on_device, mesh=finer, in_specs=placed, out_specs=P(HEADS, "blk"), check_vma=False
    )
```

profile of v0, /device:TPU:16, one launch (start us, length us, event | category | flops | bytes accessed | tf_op | source)
XLA Modules:
  0.0 239.9 jit_solution(17325042349350337519)
XLA Ops:
  7.3 0.9 copy.53
  8.2 3.7 %collective-permute-start.6 = (bf16[64,1,8,128]{3,0,2,1:T(8,128)(2,1)S(1)}, bf16[64,1,8,128]{3,0,2,1:T(8,128)(2,1)S(1)}, u32[]{:S(2)}, u32[]{:S(2)}) collective-permute-start(bf16[64,1,8,128]{3,0,2,1:T(8,128)(2,1)S(1)} %bitcast.279), channel_id=1, source_target_pairs={{0,3},{1,4},{2,5},{3,6},{4,7},{5,8},{6,9},{7,10},{8,11},{9,12},{10... | collective-permute-start | bytes 393224 | tf_op jit(solution)/shard_map/ppermute | solution.py:15
  12.0 4.3 %collective-permute-start.3 = (bf16[64,1,8,128]{3,0,2,1:T(8,128)(2,1)S(1)}, bf16[64,1,8,128]{3,0,2,1:T(8,128)(2,1)S(1)}, u32[]{:S(2)}, u32[]{:S(2)}) collective-permute-start(bf16[64,1,8,128]{3,0,2,1:T(8,128)(2,1)S(1)} %bitcast.280), channel_id=1, source_target_pairs={{0,2},{1,3},{2,4},{3,5},{4,6},{5,7},{6,8},{7,9},{8,10},{9,11},{10,... | collective-permute-start | bytes 393224 | tf_op jit(solution)/shard_map/ppermute | solution.py:15
  16.2 4.1 %collective-permute-start = (bf16[64,1,8,128]{3,0,2,1:T(8,128)(2,1)S(1)}, bf16[64,1,8,128]{3,0,2,1:T(8,128)(2,1)S(1)}, u32[]{:S(2)}, u32[]{:S(2)}) collective-permute-start(bf16[64,1,8,128]{3,0,2,1:T(8,128)(2,1)S(1)} %bitcast.281), channel_id=1, source_target_pairs={{0,1},{1,2},{2,3},{3,4},{4,5},{5,6},{6,7},{7,8},{8,9},{9,10},{10,1... | collective-permute-start | bytes 393224 | tf_op jit(solution)/shard_map/ppermute | solution.py:15
  20.4 1.3 dynamic_slice.18
  21.7 1.5 fusion.99
  23.2 1.2 iota_add_fusion.5
  24.4 1.3 iota_add_fusion.3
  26.9 1.8 fusion.9
  28.7 2.2 collective-permute-done
  31.9 1.1 fusion.14
  33.0 2.2 collective-permute-start.9
  35.2 2.1 collective-permute-start.1
  37.4 0.9 fusion.3
  38.3 1.1 fusion.16
  39.4 3.9 %collective-permute-start.10 = (f32[64,1,8]{0,2,1:T(8,128)S(1)}, f32[64,1,8]{0,2,1:T(8,128)S(1)}, u32[]{:S(2)}, u32[]{:S(2)}) collective-permute-start(f32[64,1,8]{0,2,1:T(8,128)S(1)} %bitcast.286), channel_id=1, source_target_pairs={{0,62},{1,63},{2,0},{3,1},{4,2},{5,3},{6,4},{7,5},{8,6},{9,7},{10,... | collective-permute-start | bytes 6152 | tf_op jit(solution)/shard_map/ppermute | solution.py:15
  43.3 3.5 %collective-permute-start.4 = (f32[64,1,8]{0,2,1:T(8,128)S(1)}, f32[64,1,8]{0,2,1:T(8,128)S(1)}, u32[]{:S(2)}, u32[]{:S(2)}) collective-permute-start(f32[64,1,8]{0,2,1:T(8,128)S(1)} %bitcast.283), channel_id=1, source_target_pairs={{0,62},{1,63},{2,0},{3,1},{4,2},{5,3},{6,4},{7,5},{8,6},{9,7},{10,... | collective-permute-start | bytes 6152 | tf_op jit(solution)/shard_map/ppermute | solution.py:15
  46.8 0.9 fusion
  50.4 1.1 fusion.18
  51.6 2.9 %collective-permute-start.2 = (f32[64,1,8,128]{3,0,2,1:T(8,128)S(1)}, f32[64,1,8,128]{3,0,2,1:T(8,128)S(1)}, u32[]{:S(2)}, u32[]{:S(2)}) collective-permute-start(f32[64,1,8,128]{3,0,2,1:T(8,128)S(1)} %fusion.42), channel_id=1, source_target_pairs={{0,63},{1,0},{2,1},{3,2},{4,3},{5,4},{6,5},{7,6},{8,7},{9,8},{10,9... | collective-permute-start | bytes 786440 | tf_op jit(solution)/shard_map/ppermute | solution.py:15
  54.5 3.7 %collective-permute-start.5 = (f32[64,1,8,128]{3,0,2,1:T(8,128)S(1)}, f32[64,1,8,128]{3,0,2,1:T(8,128)S(1)}, u32[]{:S(2)}, u32[]{:S(2)}) collective-permute-start(f32[64,1,8,128]{3,0,2,1:T(8,128)S(1)} %fusion.39), channel_id=1, source_target_pairs={{0,62},{1,63},{2,0},{3,1},{4,2},{5,3},{6,4},{7,5},{8,6},{9,7},{10,... | collective-permute-start | bytes 786440 | tf_op jit(solution)/shard_map/ppermute | solution.py:15
  58.2 2.4 %collective-permute-start.11 = (f32[64,1,8]{0,2,1:T(8,128)S(1)}, f32[64,1,8]{0,2,1:T(8,128)S(1)}, u32[]{:S(2)}, u32[]{:S(2)}) collective-permute-start(f32[64,1,8]{0,2,1:T(8,128)S(1)} %bitcast.287), channel_id=1, source_target_pairs={{0,61},{1,62},{2,63},{3,0},{4,1},{5,2},{6,3},{7,4},{8,5},{9,6},{10... | collective-permute-start | bytes 6152 | tf_op jit(solution)/shard_map/ppermute | solution.py:15
  60.6 2.4 collective-permute-start.7
  63.0 7.1 %collective-permute-start.8 = (f32[64,1,8,128]{3,0,2,1:T(8,128)S(1)}, f32[64,1,8,128]{3,0,2,1:T(8,128)S(1)}, u32[]{:S(2)}, u32[]{:S(2)}) collective-permute-start(f32[64,1,8,128]{3,0,2,1:T(8,128)S(1)} %fusion.36), channel_id=1, source_target_pairs={{0,61},{1,62},{2,63},{3,0},{4,1},{5,2},{6,3},{7,4},{8,5},{9,6},{10... | collective-permute-start | bytes 786440 | tf_op jit(solution)/shard_map/ppermute | solution.py:15
  70.1 1.1 fusion.12
  71.3 8.1 %collective-permute-done.8 = f32[64,1,8,128]{3,0,2,1:T(8,128)S(1)} collective-permute-done((f32[64,1,8,128]{3,0,2,1:T(8,128)S(1)}, f32[64,1,8,128]{3,0,2,1:T(8,128)S(1)}, u32[]{:S(2)}, u32[]{:S(2)}) %collective-permute-start.8) | collective-permute-done | bytes 262176 | tf_op jit(solution)/shard_map/ppermute | solution.py:15
  79.3 1.4 fusion.66
  80.9 23.8 %all_to_all.25 = bf16[2,4,8,1024]{3,2,1,0:T(8,128)(2,1)S(1)} all-to-all(bf16[2,4,8,1024]{3,2,1,0:T(8,128)(2,1)S(1)} %reshape_reshape_reshape.3), channel_id=1, replica_groups=mesh['heads_0'=2,'heads_1'=4,'blk'=64] {'heads_0'}, dimensions={0} | all-to-all | bytes 262144 | tf_op jit(solution)/shard_map/all_to_all | solution.py:34
  104.7 9.7 %all_to_all.26 = bf16[2,4,8,1024]{3,2,0,1:T(8,128)(2,1)S(1)} all-to-all(bf16[2,4,8,1024]{3,2,0,1:T(8,128)(2,1)S(1)} %copy.44), channel_id=1, replica_groups=mesh['heads_0'=2,'heads_1'=4,'blk'=64] {'heads_1'}, dimensions={1} | all-to-all | bytes 262144 | tf_op jit(solution)/shard_map/all_to_all | solution.py:34
  115.1 95.9 %all-gather.3.cloned.1.call-done = bf16[512,8192]{1,0:T(8,128)(2,1)} async-done(((bf16[8,8192]{1,0:T(8,128)(2,1)}), bf16[512,8192]{1,0:T(8,128)(2,1)}) %all-gather.3.cloned.1.call-update) | async-done | bytes 8388624 | tf_op jit(solution)/shard_map/all_gather | solution.py:108
  211.0 6.9 %convolution_convert_fusion = bf16[512,256]{1,0:T(8,128)(2,1)S(1)} fusion(bf16[512,8192]{1,0:T(8,128)(2,1)} %all-gather.3.cloned.1.call-done, bf16[8192,256]{1,0:T(8,128)(2,1)} %all-gather.5.cloned.1.call-done), kind=kOutput, calls=%fused_computation.40 | convolution fusion | flops 2147614720 | bytes 12845056 | tf_op jit(solution)/shard_map/dot_general | solution.py:107
  217.9 14.4 %all_to_all.27 = bf16[8,8,1,8,256]{4,3,1,2,0:T(8,128)(2,1)S(1)} all-to-all(bf16[8,8,1,8,256]{4,3,1,2,0:T(8,128)(2,1)S(1)} %bitcast.278), channel_id=1, replica_groups=mesh['heads_0'=2,'heads_1'=4,'blk'=64] {'heads_0','heads_1'}, dimensions={0} | all-to-all | bytes 524288 | tf_op jit(solution)/shard_map/all_to_all | solution.py:114
  (33 shorter events, 7.1 us)
Async XLA Ops:
  6.5 20.4 %copy-start = (bf16[1,2048,128]{2,1,0:T(8,128)(2,1)S(1)}, bf16[1,2048,128]{2,1,0:T(8,128)(2,1)}, u32[]{:S(2)}) copy-start(bf16[1,2048,128]{2,1,0:T(8,128)(2,1)} %param.7) | copy-start | bytes 1572868
  6.5 108.6 %all-gather.5.cloned.1.call-start = ((), (), s32[]{:S(2)}) async-start(), calls=%async_computation.4 | async-start | bytes 4718592 | tf_op jit(solution)/shard_map/all_gather | solution.py:80
  7.3 203.8 %all-gather.3.cloned.1.call-start = ((), (), s32[]{:S(2)}) async-start(), calls=%async_computation.3 | async-start | bytes 8519680 | tf_op jit(solution)/shard_map/all_gather | solution.py:108
  8.2 38.6 %collective-permute-start.6 = (bf16[64,1,8,128]{3,0,2,1:T(8,128)(2,1)S(1)}, bf16[64,1,8,128]{3,0,2,1:T(8,128)(2,1)S(1)}, u32[]{:S(2)}, u32[]{:S(2)}) collective-permute-start(bf16[64,1,8,128]{3,0,2,1:T(8,128)(2,1)S(1)} %bitcast.279), channel_id=1, source_target_pairs={{0,3},{1,4},{2,5},{3,6},{4,7},{5,8},{6,9},{7,10},{8,11},{9,12},{10... | collective-permute-start | bytes 393224 | tf_op jit(solution)/shard_map/ppermute | solution.py:15
  12.0 25.4 %collective-permute-start.3 = (bf16[64,1,8,128]{3,0,2,1:T(8,128)(2,1)S(1)}, bf16[64,1,8,128]{3,0,2,1:T(8,128)(2,1)S(1)}, u32[]{:S(2)}, u32[]{:S(2)}) collective-permute-start(bf16[64,1,8,128]{3,0,2,1:T(8,128)(2,1)S(1)} %bitcast.280), channel_id=1, source_target_pairs={{0,2},{1,3},{2,4},{3,5},{4,6},{5,7},{6,8},{7,9},{8,10},{9,11},{10,... | collective-permute-start | bytes 393224 | tf_op jit(solution)/shard_map/ppermute | solution.py:15
  16.2 14.7 %collective-permute-start = (bf16[64,1,8,128]{3,0,2,1:T(8,128)(2,1)S(1)}, bf16[64,1,8,128]{3,0,2,1:T(8,128)(2,1)S(1)}, u32[]{:S(2)}, u32[]{:S(2)}) collective-permute-start(bf16[64,1,8,128]{3,0,2,1:T(8,128)(2,1)S(1)} %bitcast.281), channel_id=1, source_target_pairs={{0,1},{1,2},{2,3},{3,4},{4,5},{5,6},{6,7},{7,8},{8,9},{9,10},{10,1... | collective-permute-start | bytes 393224 | tf_op jit(solution)/shard_map/ppermute | solution.py:15
  33.0 21.5 %collective-permute-start.9 = (f32[64,1,8]{0,2,1:T(8,128)S(1)}, f32[64,1,8]{0,2,1:T(8,128)S(1)}, u32[]{:S(2)}, u32[]{:S(2)}) collective-permute-start(f32[64,1,8]{0,2,1:T(8,128)S(1)} %bitcast.285), channel_id=1, source_target_pairs={{0,63},{1,0},{2,1},{3,2},{4,3},{5,4},{6,5},{7,6},{8,7},{9,8},{10,9... | collective-permute-start | bytes 6152 | tf_op jit(solution)/shard_map/ppermute | solution.py:15
  35.2 22.9 %collective-permute-start.1 = (f32[64,1,8]{0,2,1:T(8,128)S(1)}, f32[64,1,8]{0,2,1:T(8,128)S(1)}, u32[]{:S(2)}, u32[]{:S(2)}) collective-permute-start(f32[64,1,8]{0,2,1:T(8,128)S(1)} %bitcast.282), channel_id=1, source_target_pairs={{0,63},{1,0},{2,1},{3,2},{4,3},{5,4},{6,5},{7,6},{8,7},{9,8},{10,9... | collective-permute-start | bytes 6152 | tf_op jit(solution)/shard_map/ppermute | solution.py:15
  39.4 8.3 %copy-start.1 = (bf16[1,2048,128]{2,1,0:T(8,128)(2,1)S(1)}, bf16[1,2048,128]{2,1,0:T(8,128)(2,1)}, u32[]{:S(2)}) copy-start(bf16[1,2048,128]{2,1,0:T(8,128)(2,1)} %param.8) | copy-start | bytes 1572868
  39.4 21.2 %collective-permute-start.10 = (f32[64,1,8]{0,2,1:T(8,128)S(1)}, f32[64,1,8]{0,2,1:T(8,128)S(1)}, u32[]{:S(2)}, u32[]{:S(2)}) collective-permute-start(f32[64,1,8]{0,2,1:T(8,128)S(1)} %bitcast.286), channel_id=1, source_target_pairs={{0,62},{1,63},{2,0},{3,1},{4,2},{5,3},{6,4},{7,5},{8,6},{9,7},{10,... | collective-permute-start | bytes 6152 | tf_op jit(solution)/shard_map/ppermute | solution.py:15
  43.3 19.7 %collective-permute-start.4 = (f32[64,1,8]{0,2,1:T(8,128)S(1)}, f32[64,1,8]{0,2,1:T(8,128)S(1)}, u32[]{:S(2)}, u32[]{:S(2)}) collective-permute-start(f32[64,1,8]{0,2,1:T(8,128)S(1)} %bitcast.283), channel_id=1, source_target_pairs={{0,62},{1,63},{2,0},{3,1},{4,2},{5,3},{6,4},{7,5},{8,6},{9,7},{10,... | collective-permute-start | bytes 6152 | tf_op jit(solution)/shard_map/ppermute | solution.py:15
  51.6 19.7 %collective-permute-start.2 = (f32[64,1,8,128]{3,0,2,1:T(8,128)S(1)}, f32[64,1,8,128]{3,0,2,1:T(8,128)S(1)}, u32[]{:S(2)}, u32[]{:S(2)}) collective-permute-start(f32[64,1,8,128]{3,0,2,1:T(8,128)S(1)} %fusion.42), channel_id=1, source_target_pairs={{0,63},{1,0},{2,1},{3,2},{4,3},{5,4},{6,5},{7,6},{8,7},{9,8},{10,9... | collective-permute-start | bytes 786440 | tf_op jit(solution)/shard_map/ppermute | solution.py:15
  54.5 16.8 %collective-permute-start.5 = (f32[64,1,8,128]{3,0,2,1:T(8,128)S(1)}, f32[64,1,8,128]{3,0,2,1:T(8,128)S(1)}, u32[]{:S(2)}, u32[]{:S(2)}) collective-permute-start(f32[64,1,8,128]{3,0,2,1:T(8,128)S(1)} %fusion.39), channel_id=1, source_target_pairs={{0,62},{1,63},{2,0},{3,1},{4,2},{5,3},{6,4},{7,5},{8,6},{9,7},{10,... | collective-permute-start | bytes 786440 | tf_op jit(solution)/shard_map/ppermute | solution.py:15
  58.2 13.0 %collective-permute-start.11 = (f32[64,1,8]{0,2,1:T(8,128)S(1)}, f32[64,1,8]{0,2,1:T(8,128)S(1)}, u32[]{:S(2)}, u32[]{:S(2)}) collective-permute-start(f32[64,1,8]{0,2,1:T(8,128)S(1)} %bitcast.287), channel_id=1, source_target_pairs={{0,61},{1,62},{2,63},{3,0},{4,1},{5,2},{6,3},{7,4},{8,5},{9,6},{10... | collective-permute-start | bytes 6152 | tf_op jit(solution)/shard_map/ppermute | solution.py:15
  60.6 10.6 %collective-permute-start.7 = (f32[64,1,8]{0,2,1:T(8,128)S(1)}, f32[64,1,8]{0,2,1:T(8,128)S(1)}, u32[]{:S(2)}, u32[]{:S(2)}) collective-permute-start(f32[64,1,8]{0,2,1:T(8,128)S(1)} %bitcast.284), channel_id=1, source_target_pairs={{0,61},{1,62},{2,63},{3,0},{4,1},{5,2},{6,3},{7,4},{8,5},{9,6},{10... | collective-permute-start | bytes 6152 | tf_op jit(solution)/shard_map/ppermute | solution.py:15
  63.0 16.4 %collective-permute-start.8 = (f32[64,1,8,128]{3,0,2,1:T(8,128)S(1)}, f32[64,1,8,128]{3,0,2,1:T(8,128)S(1)}, u32[]{:S(2)}, u32[]{:S(2)}) collective-permute-start(f32[64,1,8,128]{3,0,2,1:T(8,128)S(1)} %fusion.36), channel_id=1, source_target_pairs={{0,61},{1,62},{2,63},{3,0},{4,1},{5,2},{6,3},{7,4},{8,5},{9,6},{10... | collective-permute-start | bytes 786440 | tf_op jit(solution)/shard_map/ppermute | solution.py:15
Sparse Core Ops, SparseCore 0:
  9.4 88.5 all-gather.4
  115.2 95.7 all-gather.2
where the time goes:
time: 241 us; the launch traced here: 240 us
  waiting for transfers between devices  107 us (44%)
  blocking collectives  47.9 us (20%)
  starting transfers between devices  42.3 us (18%)
  matrix products  15.5 us (6%)
  between operations  13.7 us (6%)
  other arithmetic  8.18 us (3%)
  local copies, waits for them, and re-layouts  5.26 us (2%)
    all_gather x1, waiting for transfers between devices, on_device(): lax.all_gather(share_rows, 'blk', axis=0, tiled=True)  95.9 us
    ppermute x12, starting transfers between devices, passed_along(): return lax.ppermute(value, axis, pairs)  42.3 us
    all_to_all x2, blocking collectives, exchange_in_order(): lax.all_to_all(blocks, axes[k], split_axis=k, concat_axis=k, tiled=True)  33.5 us
    all_to_all x1, blocking collectives, on_device(): lax.all_to_all(grouped, HEADS, split_axis=0, concat_axis=2, tiled=True)  14.4 us
    ppermute x12, waiting for transfers between devices, passed_along(): return lax.ppermute(value, axis, pairs)  10.3 us
    dot_general x1, matrix products, on_device(): jnp.dot(lax.all_gather(share_rows, 'blk', axis=0, tiled=True), full_weigh...  6.9 us
  transfers between devices with their start and end apart: 14, of which 3 were waited for; matrix products, arithmetic and copies ran while one was open for 9% of the time, Pallas kernels for 0%

commit v1 on v0

--- a/solution.py
+++ b/solution.py
@@ -104,10 +104,14 @@
         .reshape(query_len, heads_local * head_size)
     )
     share_rows = stepwise_exchange(attended, HEADS, (0, 1), 0, 1)
+
+    def point_thing_up(v0):
+        met_up = jnp.stack([v0 for _ in range(lax.psum(1, "blk"))])
+        now = lax.all_to_all(met_up, "blk", 0, 0)
+        return jnp.concatenate(now, axis=0)
+
     strided = jnp.dot(
-        lax.all_gather(share_rows, "blk", axis=0, tiled=True),
-        full_weight,
-        preferred_element_type=jnp.float32,
+        point_thing_up(share_rows), full_weight, preferred_element_type=jnp.float32
     ).astype(jnp.bfloat16)
     share_len = share_rows.shape[0]
     grouped = strided.reshape(group_count, shard_count // group_count, 1, share_len, columns)

time: 241 us -> 409 us (1.70)
  the two profiles are of different devices: /device:TPU:16 before, /device:TPU:272 now
where the time goes in v1:
time: 409 us; the launch traced here: 408 us
  waiting for transfers between devices  255 us (62%)
  starting transfers between devices  60.7 us (15%)
  blocking collectives  46.2 us (11%)
  matrix products  15.4 us (4%)
  between operations  13.7 us (3%)
  local copies, waits for them, and re-layouts  8.96 us (2%)
  other arithmetic  8.02 us (2%)
    all_gather x1, waiting for transfers between devices, on_device(): full_weight = lax.all_gather(w_out, HEADS, axis=0, tiled=True)  177 us
    all_to_all x1, waiting for transfers between devices, point_thing_up(): now = lax.all_to_all(met_up, 'blk', 0, 0)  68 us
    ppermute x12, starting transfers between devices, passed_along(): return lax.ppermute(value, axis, pairs)  36.1 us
    all_to_all x1, blocking collectives, on_device(): lax.all_to_all(grouped, HEADS, split_axis=0, concat_axis=2, tiled=True)  29 us
    all_to_all x1, starting transfers between devices, point_thing_up(): now = lax.all_to_all(met_up, 'blk', 0, 0)  24.5 us
    all_to_all x2, blocking collectives, exchange_in_order(): lax.all_to_all(blocks, axes[k], split_axis=k, concat_axis=k, tiled=True)  17.2 us
    ppermute x12, waiting for transfers between devices, passed_along(): return lax.ppermute(value, axis, pairs)  9.85 us
  transfers between devices with their start and end apart: 14, of which 4 were waited for; matrix products, arithmetic and copies ran while one was open for 4% of the time, Pallas kernels for 0%

profile of v1, /device:TPU:272, one launch (start us, length us, event | category | flops | bytes accessed | tf_op | source)
XLA Modules:
  0.0 408.0 jit_solution(4212525304359693174)
XLA Ops:
  7.5 3.4 collective-permute-start.3
  10.9 2.5 collective-permute-start.6
  13.5 3.8 collective-permute-start
  17.3 1.2 dynamic_slice.18
  19.2 1.5 fusion.104
  20.7 1.2 iota_add_fusion.3
  22.0 1.2 iota_add_fusion.5
  23.6 1.8 fusion.11
  27.4 1.1 fusion.18
  30.3 1.1 fusion.16
  31.4 3.7 collective-permute-start.10
  36.0 1.1 fusion.20
  37.1 1.9 collective-permute-start.11
  39.0 2.7 collective-permute-start.9
  41.8 1.9 collective-permute-start.1
  44.6 2.3 collective-permute-start.4
  46.9 3.4 collective-permute-start.7
  50.3 3.6 collective-permute-start.2
  54.0 3.4 collective-permute-start.5
  57.4 3.5 collective-permute-start.8
  60.9 1.1 fusion.14
  62.0 3.1 collective-permute-done.5
  65.1 6.8 %collective-permute-done.8 = f32[64,1,8,128]{3,0,2,1:T(8,128)S(1)} collective-permute-done((f32[64,1,8,128]{3,0,2,1:T(8,128)S(1)}, f32[64,1,8,128]{3,0,2,1:T(8,128)S(1)}, u32[]{:S(2)}, u32[]{:S(2)}) %collective-permute-start.8) | collective-permute-done | bytes 262176 | tf_op jit(solution)/shard_map/ppermute | solution.py:15
  71.9 1.4 fusion.71
  73.4 7.1 %all_to_all.30 = bf16[2,4,8,1024]{3,2,1,0:T(8,128)(2,1)S(1)} all-to-all(bf16[2,4,8,1024]{3,2,1,0:T(8,128)(2,1)S(1)} %reshape_reshape_reshape.3), channel_id=1, replica_groups=mesh['heads_0'=2,'heads_1'=4,'blk'=64] {'heads_0'}, dimensions={0} | all-to-all | bytes 262144 | tf_op jit(solution)/shard_map/all_to_all | solution.py:34
  80.5 10.1 %all_to_all.31 = bf16[2,4,8,1024]{3,2,0,1:T(8,128)(2,1)S(1)} all-to-all(bf16[2,4,8,1024]{3,2,0,1:T(8,128)(2,1)S(1)} %copy.44), channel_id=1, replica_groups=mesh['heads_0'=2,'heads_1'=4,'blk'=64] {'heads_1'}, dimensions={1} | all-to-all | bytes 262144 | tf_op jit(solution)/shard_map/all_to_all | solution.py:34
  90.6 4.2 %stack.3 = bf16[64,8,8192]{2,1,0:T(8,128)(2,1)} broadcast(bf16[8,8192]{1,0:T(8,128)(2,1)S(1)} %bitcast.281), dimensions={1,2} | broadcast | bytes 8519680 | tf_op jit(solution)/shard_map/stack | solution.py:109
  94.9 24.5 %all-to-all-start.2 = ((bf16[64,8,8192]{2,1,0:T(8,128)(2,1)}), bf16[64,8,8192]{2,1,0:T(8,128)(2,1)}, u32[]{:S(2)}, u32[]{:S(2)}) async-start(bf16[64,8,8192]{2,1,0:T(8,128)(2,1)} %stack.3), calls=%async_computation.2 | async-start | bytes 16777216 | tf_op jit(solution)/shard_map/all_to_all | solution.py:110
  120.1 176.5 %all-gather.2.cloned.1.call-done = bf16[8192,256]{1,0:T(8,128)(2,1)} async-done(((bf16[1024,256]{1,0:T(8,128)(2,1)}), bf16[8192,256]{1,0:T(8,128)(2,1)}) %all-gather.2.cloned.1.call-update) | async-done | bytes 4194320 | tf_op jit(solution)/shard_map/all_gather | solution.py:80
  296.6 68.0 %all-to-all-done.2 = bf16[64,8,8192]{2,1,0:T(8,128)(2,1)} async-done(((bf16[64,8,8192]{2,1,0:T(8,128)(2,1)}), bf16[64,8,8192]{2,1,0:T(8,128)(2,1)}, u32[]{:S(2)}, u32[]{:S(2)}) %all-to-all-start.2) | async-done | bytes 8388640 | tf_op jit(solution)/shard_map/all_to_all | solution.py:110
  364.5 6.9 %fusion.38 = bf16[512,256]{1,0:T(8,128)(2,1)S(1)} fusion(bf16[8192,256]{1,0:T(8,128)(2,1)} %all-gather.2.cloned.1.call-done, bf16[64,8,8192]{2,1,0:T(8,128)(2,1)} %all-to-all-done.2), kind=kOutput, calls=%fused_computation.42 | convolution fusion | flops 2147614720 | bytes 12845056 | tf_op jit(solution)/shard_map/dot_general | solution.py:113
  371.4 29.0 %all_to_all.32 = bf16[8,8,1,8,256]{4,3,1,2,0:T(8,128)(2,1)S(1)} all-to-all(bf16[8,8,1,8,256]{4,3,1,2,0:T(8,128)(2,1)S(1)} %bitcast.282), channel_id=1, replica_groups=mesh['heads_0'=2,'heads_1'=4,'blk'=64] {'heads_0','heads_1'}, dimensions={0} | all-to-all | bytes 524288 | tf_op jit(solution)/shard_map/all_to_all | solution.py:118
  (33 shorter events, 9.2 us)
Async XLA Ops:
  6.5 17.1 %copy-start = (bf16[1,2048,128]{2,1,0:T(8,128)(2,1)S(1)}, bf16[1,2048,128]{2,1,0:T(8,128)(2,1)}, u32[]{:S(2)}) copy-start(bf16[1,2048,128]{2,1,0:T(8,128)(2,1)} %param.7) | copy-start | bytes 1572868
  7.5 18.0 %collective-permute-start.3 = (bf16[64,1,8,128]{3,0,2,1:T(8,128)(2,1)S(1)}, bf16[64,1,8,128]{3,0,2,1:T(8,128)(2,1)S(1)}, u32[]{:S(2)}, u32[]{:S(2)}) collective-permute-start(bf16[64,1,8,128]{3,0,2,1:T(8,128)(2,1)S(1)} %bitcast.283), channel_id=1, source_target_pairs={{0,2},{1,3},{2,4},{3,5},{4,6},{5,7},{6,8},{7,9},{8,10},{9,11},{10,... | collective-permute-start | bytes 393224 | tf_op jit(solution)/shard_map/ppermute | solution.py:15
  10.9 24.2 %collective-permute-start.6 = (bf16[64,1,8,128]{3,0,2,1:T(8,128)(2,1)S(1)}, bf16[64,1,8,128]{3,0,2,1:T(8,128)(2,1)S(1)}, u32[]{:S(2)}, u32[]{:S(2)}) collective-permute-start(bf16[64,1,8,128]{3,0,2,1:T(8,128)(2,1)S(1)} %bitcast.284), channel_id=1, source_target_pairs={{0,3},{1,4},{2,5},{3,6},{4,7},{5,8},{6,9},{7,10},{8,11},{9,12},{10... | collective-permute-start | bytes 393224 | tf_op jit(solution)/shard_map/ppermute | solution.py:15
  13.5 15.0 %collective-permute-start = (bf16[64,1,8,128]{3,0,2,1:T(8,128)(2,1)S(1)}, bf16[64,1,8,128]{3,0,2,1:T(8,128)(2,1)S(1)}, u32[]{:S(2)}, u32[]{:S(2)}) collective-permute-start(bf16[64,1,8,128]{3,0,2,1:T(8,128)(2,1)S(1)} %bitcast.285), channel_id=1, source_target_pairs={{0,1},{1,2},{2,3},{3,4},{4,5},{5,6},{6,7},{7,8},{8,9},{9,10},{10,1... | collective-permute-start | bytes 393224 | tf_op jit(solution)/shard_map/ppermute | solution.py:15
  25.5 1.0 copy-start.1
  31.4 15.5 %collective-permute-start.10 = (f32[64,1,8]{0,2,1:T(8,128)S(1)}, f32[64,1,8]{0,2,1:T(8,128)S(1)}, u32[]{:S(2)}, u32[]{:S(2)}) collective-permute-start(f32[64,1,8]{0,2,1:T(8,128)S(1)} %bitcast.290), channel_id=1, source_target_pairs={{0,62},{1,63},{2,0},{3,1},{4,2},{5,3},{6,4},{7,5},{8,6},{9,7},{10,... | collective-permute-start | bytes 6152 | tf_op jit(solution)/shard_map/ppermute | solution.py:15
  37.1 13.2 %collective-permute-start.11 = (f32[64,1,8]{0,2,1:T(8,128)S(1)}, f32[64,1,8]{0,2,1:T(8,128)S(1)}, u32[]{:S(2)}, u32[]{:S(2)}) collective-permute-start(f32[64,1,8]{0,2,1:T(8,128)S(1)} %bitcast.291), channel_id=1, source_target_pairs={{0,61},{1,62},{2,63},{3,0},{4,1},{5,2},{6,3},{7,4},{8,5},{9,6},{10... | collective-permute-start | bytes 6152 | tf_op jit(solution)/shard_map/ppermute | solution.py:15
  39.0 14.9 %collective-permute-start.9 = (f32[64,1,8]{0,2,1:T(8,128)S(1)}, f32[64,1,8]{0,2,1:T(8,128)S(1)}, u32[]{:S(2)}, u32[]{:S(2)}) collective-permute-start(f32[64,1,8]{0,2,1:T(8,128)S(1)} %bitcast.289), channel_id=1, source_target_pairs={{0,63},{1,0},{2,1},{3,2},{4,3},{5,4},{6,5},{7,6},{8,7},{9,8},{10,9... | collective-permute-start | bytes 6152 | tf_op jit(solution)/shard_map/ppermute | solution.py:15
  41.8 15.6 %collective-permute-start.1 = (f32[64,1,8]{0,2,1:T(8,128)S(1)}, f32[64,1,8]{0,2,1:T(8,128)S(1)}, u32[]{:S(2)}, u32[]{:S(2)}) collective-permute-start(f32[64,1,8]{0,2,1:T(8,128)S(1)} %bitcast.287), channel_id=1, source_target_pairs={{0,63},{1,0},{2,1},{3,2},{4,3},{5,4},{6,5},{7,6},{8,7},{9,8},{10,9... | collective-permute-start | bytes 6152 | tf_op jit(solution)/shard_map/ppermute | solution.py:15
  44.6 17.4 %collective-permute-start.4 = (f32[64,1,8]{0,2,1:T(8,128)S(1)}, f32[64,1,8]{0,2,1:T(8,128)S(1)}, u32[]{:S(2)}, u32[]{:S(2)}) collective-permute-start(f32[64,1,8]{0,2,1:T(8,128)S(1)} %bitcast.286), channel_id=1, source_target_pairs={{0,62},{1,63},{2,0},{3,1},{4,2},{5,3},{6,4},{7,5},{8,6},{9,7},{10,... | collective-permute-start | bytes 6152 | tf_op jit(solution)/shard_map/ppermute | solution.py:15
  46.9 15.1 %collective-permute-start.7 = (f32[64,1,8]{0,2,1:T(8,128)S(1)}, f32[64,1,8]{0,2,1:T(8,128)S(1)}, u32[]{:S(2)}, u32[]{:S(2)}) collective-permute-start(f32[64,1,8]{0,2,1:T(8,128)S(1)} %bitcast.288), channel_id=1, source_target_pairs={{0,61},{1,62},{2,63},{3,0},{4,1},{5,2},{6,3},{7,4},{8,5},{9,6},{10... | collective-permute-start | bytes 6152 | tf_op jit(solution)/shard_map/ppermute | solution.py:15
  50.3 11.7 %collective-permute-start.2 = (f32[64,1,8,128]{3,0,2,1:T(8,128)S(1)}, f32[64,1,8,128]{3,0,2,1:T(8,128)S(1)}, u32[]{:S(2)}, u32[]{:S(2)}) collective-permute-start(f32[64,1,8,128]{3,0,2,1:T(8,128)S(1)} %fusion.47), channel_id=1, source_target_pairs={{0,63},{1,0},{2,1},{3,2},{4,3},{5,4},{6,5},{7,6},{8,7},{9,8},{10,9... | collective-permute-start | bytes 786440 | tf_op jit(solution)/shard_map/ppermute | solution.py:15
  54.0 11.1 %collective-permute-start.5 = (f32[64,1,8,128]{3,0,2,1:T(8,128)S(1)}, f32[64,1,8,128]{3,0,2,1:T(8,128)S(1)}, u32[]{:S(2)}, u32[]{:S(2)}) collective-permute-start(f32[64,1,8,128]{3,0,2,1:T(8,128)S(1)} %fusion.44), channel_id=1, source_target_pairs={{0,62},{1,63},{2,0},{3,1},{4,2},{5,3},{6,4},{7,5},{8,6},{9,7},{10,... | collective-permute-start | bytes 786440 | tf_op jit(solution)/shard_map/ppermute | solution.py:15
  57.4 14.5 %collective-permute-start.8 = (f32[64,1,8,128]{3,0,2,1:T(8,128)S(1)}, f32[64,1,8,128]{3,0,2,1:T(8,128)S(1)}, u32[]{:S(2)}, u32[]{:S(2)}) collective-permute-start(f32[64,1,8,128]{3,0,2,1:T(8,128)S(1)} %fusion.41), channel_id=1, source_target_pairs={{0,61},{1,62},{2,63},{3,0},{4,1},{5,2},{6,3},{7,4},{8,5},{9,6},{10... | collective-permute-start | bytes 786440 | tf_op jit(solution)/shard_map/ppermute | solution.py:15
  94.9 269.7 %all-to-all-start.2 = ((bf16[64,8,8192]{2,1,0:T(8,128)(2,1)}), bf16[64,8,8192]{2,1,0:T(8,128)(2,1)}, u32[]{:S(2)}, u32[]{:S(2)}) async-start(bf16[64,8,8192]{2,1,0:T(8,128)(2,1)} %stack.3), calls=%async_computation.2 | async-start | bytes 16777216 | tf_op jit(solution)/shard_map/all_to_all | solution.py:110
  119.3 177.2 %all-gather.2.cloned.1.call-start = ((), (), s32[]{:S(2)}) async-start(), calls=%async_computation.4 | async-start | bytes 4718592 | tf_op jit(solution)/shard_map/all_gather | solution.py:80
Sparse Core Ops, SparseCore 0:
  122.2 174.3 all-gather.1
